TPU v7x, 32 devices: a whole 2x2x4 slice. The times are simulated.
32 devices in a mesh: dp: 8 (over y, x, core), tensor: 4 (over z).
Axes of the slice: x: 2, y: 2, z: 4, core: 2. Of those that a mesh axis runs over, the one named last changes fastest.
Arguments:
- tokens: bfloat16 [32, 256, 1152], P(('dp', 'tensor')), may hold values from -6 to 6
- timesteps: int32 [32], P('dp'), may hold values from 0 to 999
- labels: int32 [32], P('dp'), may hold values from 0 to 999
- item_counts: int32 [8], P('dp'), may hold values from 1 to 4
- cotangent: bfloat16 [32, 256, 1152], P(('dp', 'tensor')), may hold values from -6 to 6
- project_weight: bfloat16 [1152, 3, 1152], P(None, None, 'tensor'), may hold values from -0.1875 to 0.1875
- query_gain: bfloat16 [72], replicated, may hold values from 0.099609375 to 1.8984375
- key_gain: bfloat16 [72], replicated, may hold values from 0.099609375 to 1.8984375
- output_weight: bfloat16 [1152, 1152], P('tensor'), may hold values from -0.5 to 0.5
- output_bias: bfloat16 [1152], replicated, may hold values from -3 to 3
- expand_weight: bfloat16 [1152, 2, 3072], P(None, None, 'tensor'), may hold values from -0.1875 to 0.1875
- down_weight: bfloat16 [3072, 1152], P('tensor'), may hold values from -0.15625 to 0.15625
- down_bias: bfloat16 [1152], replicated, may hold values from -3 to 3
- modulate_weight: bfloat16 [1152, 6, 1152], P(None, None, 'tensor'), may hold values from -0.1875 to 0.1875
- modulate_bias: bfloat16 [6, 1152], P(None, 'tensor'), may hold values from -3 to 3
- time_weight: bfloat16 [256, 1152], replicated, may hold values from -0.5 to 0.5
- time_bias: bfloat16 [1152], replicated, may hold values from -3 to 3
- embed_weight: bfloat16 [1152, 1152], replicated, may hold values from -0.25 to 0.25
- embed_bias: bfloat16 [1152], replicated, may hold values from -3 to 3
- class_table: bfloat16 [1000, 1152], replicated, may hold values from -6 to 6
Outputs:
- result: bfloat16 [32, 256, 1152], P(('dp', 'tensor'))
- tokens_grad: bfloat16 [32, 256, 1152], P(('dp', 'tensor'))
- project_grad: float32 [1152, 3, 1152], P('dp', None, 'tensor')
- query_gain_grad: float32 [72], replicated
- key_gain_grad: float32 [72], replicated
- output_weight_grad: float32 [1152, 1152], P('tensor', 'dp')
- output_bias_grad: float32 [1152], replicated
- expand_grad: float32 [1152, 2, 3072], P('dp', None, 'tensor')
- down_grad: float32 [3072, 1152], P('tensor', 'dp')
- down_bias_grad: float32 [1152], replicated
- modulate_grad: float32 [1152, 6, 1152], P('dp', None, 'tensor')
- modulate_bias_grad: float32 [6, 1152], replicated
- time_grad: float32 [256, 1152], P(None, 'dp')
- time_bias_grad: float32 [1152], P('dp')
- embed_grad: float32 [1152, 1152], P('dp')
- embed_bias_grad: float32 [1152], P('dp')
- class_grad: float32 [1000, 1152], P(None, 'dp')
Inputs may be any that keep to these rules, and one draw needn't show every extreme that they name: `item_counts`: entry i counts the real items among the 4 items of index i of dp; they are its first ones.
All inputs are finite; a program needn't handle non-finite values.
Results may differ from a plain program's by a relative error of at most 0.03.
Values may be sent and summed in bfloat16 or wider, within the bound.
A program may use at most 256 MiB of HBM per device.

v0:
```python
import math
import jax
import jax.numpy as jnp
from jax import lax
from jax.sharding import PartitionSpec as P

HD = 72
FREQ = 256
GRID = 16
EPS = 1e-06


def layer_norm(value):
    center = value - jnp.mean(value, axis=-1, keepdims=True)
    inverse = lax.rsqrt(jnp.mean(center * center, axis=-1, keepdims=True) + EPS)
    return (center * inverse, inverse)


def layer_norm_back(normed, inverse, grad):
    return inverse * (
        grad
        - jnp.mean(grad, axis=-1, keepdims=True)
        - normed * jnp.mean(grad * normed, axis=-1, keepdims=True)
    )


def silu_slope(value):
    sigma = jax.nn.sigmoid(value)
    return sigma * (1.0 + value * (1.0 - sigma))


def rotate(value, positions):
    quarter = HD // 4
    rates = 10000.0 ** (-jnp.arange(quarter, dtype=jnp.float32) / quarter)
    places = ((positions // GRID).astype(jnp.float32), (positions % GRID).astype(jnp.float32))
    pieces = []
    for which_half in range(2):
        half_value = value[..., which_half * 2 * quarter : (which_half + 1) * 2 * quarter]
        angle = places[which_half][:, None] * rates[None, :]
        cosine = jnp.cos(angle)[None, :, None, :]
        sine = jnp.sin(angle)[None, :, None, :]
        first = half_value[..., :quarter]
        second = half_value[..., quarter:]
        pieces.append(first * cosine - second * sine)
        pieces.append(second * cosine + first * sine)
    return jnp.concatenate(pieces, axis=-1)


def head_prepare(raw, gain, positions):
    scaled = raw * lax.rsqrt(jnp.mean(raw * raw, axis=-1, keepdims=True) + EPS) * gain
    return rotate(scaled, positions)


def time_features(steps_in):
    half = FREQ // 2
    rates = jnp.exp(-math.log(10000.0) * jnp.arange(half, dtype=jnp.float32) / half)
    angle = steps_in.astype(jnp.float32)[:, None] * rates[None, :]
    return jnp.concatenate([jnp.cos(angle), jnp.sin(angle)], axis=-1)


def shards(
    tokens,
    timesteps,
    labels,
    item_counts,
    cotangent,
    project_weight,
    query_gain,
    key_gain,
    output_weight,
    output_bias,
    expand_weight,
    down_weight,
    down_bias,
    modulate_weight,
    modulate_bias,
    time_weight,
    time_bias,
    embed_weight,
    embed_bias,
    class_table,
):
    local_items, length, width = tokens.shape
    items = timesteps.shape[0]
    slab = modulate_weight.shape[2]
    heads_here = project_weight.shape[2] // HD
    scale = HD ** (-0.5)
    lane = lax.axis_index("tensor")
    first_item = lane * local_items
    live = (first_item + jnp.arange(local_items) < item_counts[0]).astype(jnp.float32)[
        :, None, None
    ]
    index = lax.axis_index("dp")
    tags = lax.all_gather(jnp.stack([timesteps, labels]), "dp", axis=1, tiled=True)
    time_feat = time_features(tags[0]).astype(jnp.bfloat16)
    pre_hidden = jnp.dot(
        time_feat, time_weight, preferred_element_type=jnp.float32
    ) + time_bias.astype(jnp.float32)
    time_hidden = jax.nn.silu(pre_hidden).astype(jnp.bfloat16)
    condition = (
        jnp.dot(time_hidden, embed_weight, preferred_element_type=jnp.float32)
        + embed_bias.astype(jnp.float32)
        + jnp.take(class_table, tags[1], axis=0).astype(jnp.float32)
    )
    cond_act = jax.nn.silu(condition).astype(jnp.bfloat16)
    cond_act_here = lax.dynamic_slice_in_dim(cond_act, index * items, items, 0)
    condition_here = lax.dynamic_slice_in_dim(condition, index * items, items, 0)
    modulation_part = (
        jnp.einsum(
            "bd,dke->bke", cond_act_here, modulate_weight, preferred_element_type=jnp.float32
        )
        + modulate_bias.astype(jnp.float32)
    ).astype(jnp.bfloat16)
    modulation_local = lax.all_to_all(
        modulation_part, "tensor", split_axis=0, concat_axis=2, tiled=True
    ).astype(jnp.float32)
    local_parts = [modulation_local[:, which][:, None, :] for which in range(6)]
    attend_shift, attend_scale, attend_gate, feed_shift, feed_scale, feed_gate = local_parts
    positions = jnp.arange(length)
    token_local = tokens.astype(jnp.float32)
    normed_local, inverse_local = layer_norm(token_local)
    mod_in = lax.all_gather(
        (normed_local * (1.0 + attend_scale) + attend_shift).astype(jnp.bfloat16),
        "tensor",
        axis=0,
        tiled=True,
    )
    projected = jnp.einsum(
        "bld,dke->blke", mod_in, project_weight, preferred_element_type=jnp.float32
    )
    split = projected.reshape(items, length, 3, heads_here, HD)
    query_gain_f = query_gain.astype(jnp.float32)
    key_gain_f = key_gain.astype(jnp.float32)
    queries = head_prepare(split[:, :, 0], query_gain_f, positions).astype(jnp.bfloat16)
    keys = head_prepare(split[:, :, 1], key_gain_f, positions).astype(jnp.bfloat16)
    values = split[:, :, 2].astype(jnp.bfloat16)
    scores = (
        jnp.einsum("bqhd,bkhd->bhqk", queries, keys, preferred_element_type=jnp.float32) * scale
    )
    top = jnp.max(scores, axis=-1, keepdims=True)
    logsum = top + jnp.log(jnp.sum(jnp.exp(scores - top), axis=-1, keepdims=True))
    probs = jnp.exp(scores - logsum).astype(jnp.bfloat16)
    mixed = jnp.einsum("bhqk,bkhd->bqhd", probs, values, preferred_element_type=jnp.float32)
    mixed = mixed.reshape(items, length, heads_here * HD).astype(jnp.bfloat16)
    piece = mixed
    attend_branch = lax.psum_scatter(
        jnp.einsum("blh,hd->bld", piece, output_weight, preferred_element_type=jnp.float32).astype(
            jnp.bfloat16
        ),
        "tensor",
        scatter_dimension=0,
        tiled=True,
    ).astype(jnp.float32) + output_bias.astype(jnp.float32)
    residual = token_local + attend_gate * attend_branch
    normed_two, inverse_two = layer_norm(residual)
    mod_two = (normed_two * (1.0 + feed_scale) + feed_shift).astype(jnp.bfloat16)
    mod_two_all = lax.all_gather(mod_two, "tensor", axis=0, tiled=True)
    gate_up = jnp.einsum(
        "bld,dkf->blkf", mod_two_all, expand_weight, preferred_element_type=jnp.float32
    )
    gate = gate_up[:, :, 0]
    upper = gate_up[:, :, 1]
    hidden = (jax.nn.silu(gate) * upper).astype(jnp.bfloat16)
    piece = hidden
    feed_branch = lax.psum_scatter(
        jnp.einsum("blf,fd->bld", piece, down_weight, preferred_element_type=jnp.float32).astype(
            jnp.bfloat16
        ),
        "tensor",
        scatter_dimension=0,
        tiled=True,
    ).astype(jnp.float32) + down_bias.astype(jnp.float32)
    result = (live * (residual + feed_gate * feed_branch)).astype(jnp.bfloat16)
    out_grad = cotangent.astype(jnp.float32) * live
    branch_grad = (out_grad * feed_gate).astype(jnp.bfloat16)
    down_bias_part = jnp.sum(branch_grad.astype(jnp.float32), axis=(0, 1))
    piece = lax.all_gather(branch_grad, "tensor", axis=0, tiled=True)
    weight_total = jnp.einsum("blf,bld->fd", hidden, piece, preferred_element_type=jnp.float32)
    rows_grad = jnp.einsum("bld,fd->blf", piece, down_weight, preferred_element_type=jnp.float32)
    hidden_total = rows_grad
    down_grad = weight_total
    gate_up_grad = jnp.stack(
        [hidden_total * upper * silu_slope(gate), hidden_total * jax.nn.silu(gate)], axis=2
    ).astype(jnp.bfloat16)
    expand_grad = jnp.einsum(
        "bld,blkf->dkf", mod_two_all, gate_up_grad, preferred_element_type=jnp.float32
    )
    piece = gate_up_grad
    mod_two_grad = lax.psum_scatter(
        jnp.einsum(
            "blkf,dkf->bld", piece, expand_weight, preferred_element_type=jnp.float32
        ).astype(jnp.bfloat16),
        "tensor",
        scatter_dimension=0,
        tiled=True,
    ).astype(jnp.float32)
    residual_grad = out_grad + layer_norm_back(
        normed_two, inverse_two, mod_two_grad * (1.0 + feed_scale)
    )
    attend_grad = (residual_grad * attend_gate).astype(jnp.bfloat16)
    output_bias_part = jnp.sum(attend_grad.astype(jnp.float32), axis=(0, 1))
    piece = lax.all_gather(attend_grad, "tensor", axis=0, tiled=True)
    weight_total = jnp.einsum("blh,bld->hd", mixed, piece, preferred_element_type=jnp.float32)
    rows_grad = jnp.einsum("bld,hd->blh", piece, output_weight, preferred_element_type=jnp.float32)
    output_weight_grad = weight_total
    mixed_grad = rows_grad
    mixed_grad = mixed_grad.reshape(items, length, heads_here, HD).astype(jnp.bfloat16)
    again = jnp.einsum("bqhd,bkhd->bhqk", queries, keys, preferred_element_type=jnp.float32) * scale
    prob_float = jnp.exp(again - logsum)
    prob_low = prob_float.astype(jnp.bfloat16)
    prob_grad = jnp.einsum(
        "bqhd,bkhd->bhqk", mixed_grad, values, preferred_element_type=jnp.float32
    )
    score_grad = (
        prob_float * (prob_grad - jnp.sum(prob_float * prob_grad, axis=-1, keepdims=True))
    ).astype(jnp.bfloat16)
    query_grad = (
        jnp.einsum("bhqk,bkhd->bqhd", score_grad, keys, preferred_element_type=jnp.float32) * scale
    )
    key_grad = (
        jnp.einsum("bhqk,bqhd->bkhd", score_grad, queries, preferred_element_type=jnp.float32)
        * scale
    )
    value_grad = jnp.einsum(
        "bhqk,bqhd->bkhd", prob_low, mixed_grad, preferred_element_type=jnp.float32
    )

    def prepare_here(raw, gain):
        return head_prepare(raw, gain, positions)

    _, query_back = jax.vjp(prepare_here, split[:, :, 0], query_gain_f)
    raw_query_grad, query_gain_part = query_back(query_grad)
    _, key_back = jax.vjp(prepare_here, split[:, :, 1], key_gain_f)
    raw_key_grad, key_gain_part = key_back(key_grad)
    projected_grad = jnp.stack([raw_query_grad, raw_key_grad, value_grad], axis=2)
    projected_grad = projected_grad.reshape(items, length, 3, heads_here * HD).astype(jnp.bfloat16)
    project_grad = jnp.einsum(
        "bld,blke->dke", mod_in, projected_grad, preferred_element_type=jnp.float32
    )
    piece = projected_grad
    mod_in_grad = lax.psum_scatter(
        jnp.einsum(
            "blke,dke->bld", piece, project_weight, preferred_element_type=jnp.float32
        ).astype(jnp.bfloat16),
        "tensor",
        scatter_dimension=0,
        tiled=True,
    ).astype(jnp.float32)
    tokens_grad = (
        residual_grad
        + layer_norm_back(normed_local, inverse_local, mod_in_grad * (1.0 + attend_scale))
    ).astype(jnp.bfloat16)
    modulation_grad_part = jnp.stack(
        [
            jnp.sum(mod_in_grad, axis=1),
            jnp.sum(mod_in_grad * normed_local, axis=1),
            jnp.sum(residual_grad * attend_branch, axis=1),
            jnp.sum(mod_two_grad, axis=1),
            jnp.sum(mod_two_grad * normed_two, axis=1),
            jnp.sum(out_grad * feed_branch, axis=1),
        ],
        axis=1,
    )
    modulation_grad = lax.all_to_all(
        modulation_grad_part, "tensor", split_axis=2, concat_axis=0, tiled=True
    ).astype(jnp.bfloat16)
    modulate_bias_part = jnp.sum(modulation_grad.astype(jnp.float32), axis=0)
    cond_part = jnp.einsum(
        "bke,dke->bd", modulation_grad, modulate_weight, preferred_element_type=jnp.float32
    )
    cond_total = lax.psum(cond_part, "tensor")
    cond_grad_here = (cond_total * silu_slope(condition_here)).astype(jnp.bfloat16)
    packed = jnp.concatenate([cond_grad_here, modulation_grad.reshape(items, 6 * slab)], axis=1)
    packed = lax.all_gather(packed, "dp", axis=0, tiled=True)
    cond_grad = packed[:, :width]
    modulation_grad_all = packed[:, width:].reshape(-1, 6, slab)
    share = width // lax.axis_size("dp")

    def mine(value, axis):
        return lax.dynamic_slice_in_dim(value, index * share, share, axis)

    one_hot = (tags[1][:, None] == jnp.arange(class_table.shape[0])[None, :]).astype(jnp.bfloat16)
    cond_grad_mine = mine(cond_grad, 1)
    class_grad = jnp.einsum(
        "bc,bd->cd", one_hot, cond_grad_mine, preferred_element_type=jnp.float32
    )
    pre_grad = (
        jnp.einsum(
            "be,de->bd", cond_grad, mine(embed_weight, 0), preferred_element_type=jnp.float32
        )
        * silu_slope(mine(pre_hidden, 1))
    ).astype(jnp.bfloat16)
    modulate_grad = jnp.einsum(
        "bd,bke->dke", mine(cond_act, 1), modulation_grad_all, preferred_element_type=jnp.float32
    )
    embed_grad = jnp.einsum(
        "bd,be->de", mine(time_hidden, 1), cond_grad, preferred_element_type=jnp.float32
    )
    embed_bias_grad = jnp.sum(cond_grad_mine.astype(jnp.float32), axis=0)
    time_grad = jnp.einsum("bf,bd->fd", time_feat, pre_grad, preferred_element_type=jnp.float32)
    time_bias_grad = jnp.sum(pre_grad.astype(jnp.float32), axis=0)
    bias_wide = lax.dynamic_update_slice_in_dim(
        jnp.zeros((6, width), jnp.float32), modulate_bias_part, lane * slab, 1
    )
    small = jnp.concatenate(
        [output_bias_part, down_bias_part, bias_wide.reshape(-1), query_gain_part, key_gain_part]
    )
    small = lax.psum(small, ("dp", "tensor"))
    output_bias_grad = small[:width]
    down_bias_grad = small[width : 2 * width]
    modulate_bias_grad = small[2 * width : 8 * width].reshape(6, width)
    query_gain_grad = small[8 * width : 8 * width + HD]
    key_gain_grad = small[8 * width + HD :]

    def scatter(value, axis):
        value = value.astype(jnp.bfloat16)
        return lax.psum_scatter(value, "dp", scatter_dimension=axis, tiled=True).astype(jnp.float32)

    project_grad = scatter(project_grad, 0)
    output_weight_grad = scatter(output_weight_grad, 1)
    expand_grad = scatter(expand_grad, 0)
    down_grad = scatter(down_grad, 1)
    return (
        result,
        tokens_grad,
        project_grad,
        query_gain_grad,
        key_gain_grad,
        output_weight_grad,
        output_bias_grad,
        expand_grad,
        down_grad,
        down_bias_grad,
        modulate_grad,
        modulate_bias_grad,
        time_grad,
        time_bias_grad,
        embed_grad,
        embed_bias_grad,
        class_grad,
    )


def solution(mesh):
    return jax.shard_map(
        shards,
        mesh=mesh,
        in_specs=(
            P(("dp", "tensor"), None, None),
            P("dp"),
            P("dp"),
            P("dp"),
            P(("dp", "tensor"), None, None),
            P(None, None, "tensor"),
            P(),
            P(),
            P("tensor", None),
            P(),
            P(None, None, "tensor"),
            P("tensor", None),
            P(),
            P(None, None, "tensor"),
            P(None, "tensor"),
            P(),
            P(),
            P(),
            P(),
            P(),
        ),
        out_specs=(
            P(("dp", "tensor"), None, None),
            P(("dp", "tensor"), None, None),
            P("dp", None, "tensor"),
            P(),
            P(),
            P("tensor", "dp"),
            P(),
            P("dp", None, "tensor"),
            P("tensor", "dp"),
            P(),
            P("dp", None, "tensor"),
            P(),
            P(None, "dp"),
            P("dp"),
            P("dp", None),
            P("dp"),
            P(None, "dp"),
        ),
        check_vma=False,
    )
```

profile of v0, /device:TPU:0, one launch (start us, length us, event | category | flops | bytes accessed | tf_op | source)
XLA Modules:
  0.0 764.2 jit_solution(1192706459011180409)
XLA Ops:
  8.1 10.4 %all-gather = s32[8,4,2]{1,2,0:T(2,128)S(1)} all-gather(s32[1,4,2]{1,2,0:T(2,128)S(1)} %add_bitcast_fusion), channel_id=1, replica_groups=mesh['dp'=8,'tensor'=4] {'dp'}, dimensions={0}, use_global_device_ids=true | all-gather | bytes 288 | tf_op jit(solution)/shard_map/all_gather | solution.py:94
  29.4 4.9 all-to-all-start
  34.8 5.1 all-to-all-done
  42.8 47.1 %all-gather.7.cloned.1.call-done = bf16[4,256,1152]{2,1,0:T(8,128)(2,1)} async-done(((bf16[1,256,1152]{2,1,0:T(8,128)(2,1)}), bf16[4,256,1152]{2,1,0:T(8,128)(2,1)}) %all-gather.7.cloned.1.call-update) | async-done | bytes 2359312 | tf_op jit(solution)/shard_map/all_gather | solution.py:122
  90.0 4.7 fusion.10
  107.8 45.3 %reduce-scatter.9.cloned.1.call-done = bf16[1,256,1152]{2,1,0:T(8,128)(2,1)} async-done(((bf16[4,256,1152]{2,1,0:T(8,128)(2,1)}), bf16[1,256,1152]{2,1,0:T(8,128)(2,1)}) %reduce-scatter.9.cloned.1.call-update) | async-done | bytes 589840 | tf_op jit(solution)/shard_map/reduce_scatter | solution.py:146
  160.6 45.8 %all-gather.9.cloned.1.call-done = bf16[4,256,1152]{2,1,0:T(8,128)(2,1)} async-done(((bf16[1,256,1152]{2,1,0:T(8,128)(2,1)}), bf16[4,256,1152]{2,1,0:T(8,128)(2,1)}) %all-gather.9.cloned.1.call-update) | async-done | bytes 2359312 | tf_op jit(solution)/shard_map/all_gather | solution.py:157
  206.4 9.6 %fusion.1 = f32[4,256,2,768]{3,1,2,0:T(8,128)} fusion(bf16[1152,2,768]{2,1,0:T(2,128)(2,1)} %param.30, bf16[4,256,1152]{2,1,0:T(8,128)(2,1)} %all-gather.9.cloned.1.call-done), kind=kOutput, calls=%fused_computation.14 | convolution fusion | flops 3623878656 | bytes 12189696 | tf_op jit(solution)/shard_map/bld,dkf->blkf/dot_general | solution.py:158
  216.0 41.2 %all-gather.11.cloned.1.call-done = bf16[4,256,1152]{2,1,0:T(8,128)(2,1)} async-done(((bf16[1,256,1152]{2,1,0:T(8,128)(2,1)}), bf16[4,256,1152]{2,1,0:T(8,128)(2,1)}) %all-gather.11.cloned.1.call-update) | async-done | bytes 2359312 | tf_op jit(solution)/shard_map/all_gather | solution.py:177
  257.2 8.4 %fusion.26 = (bf16[4,256,1,768]{3,1,0,2:T(8,128)(2,1)S(1)}, bf16[4,256,1,768]{3,1,0,2:T(8,128)(2,1)S(1)}, bf16[4,256,768]{2,1,0:T(8,128)(2,1)}) fusion(f32[4,256,2,768]{3,1,2,0:T(8,128)} %fusion.1, bf16[4,256,1152]{2,1,0:T(8,128)(2,1)} %all-gather.11.cloned.1.call-done, bf16[768,1152]{1,0:T(8,128)(2,1)} %param.31), kind=kOutput, calls=%fused_computation.62 | convolution fusion | flops 1823735808 | bytes 15138816 | tf_op jit(solution)/shard_map/bld,fd->blf/dot_general | solution.py:179
  267.2 5.6 bitcast_convert_fusion.3
  272.8 5.6 convolution_convert_fusion
  279.8 39.6 %reduce-scatter.13.cloned.1.call-done = bf16[1,256,1152]{2,1,0:T(8,128)(2,1)} async-done(((bf16[4,256,1152]{2,1,0:T(8,128)(2,1)}), bf16[1,256,1152]{2,1,0:T(8,128)(2,1)}) %reduce-scatter.13.cloned.1.call-update) | async-done | bytes 589840 | tf_op jit(solution)/shard_map/reduce_scatter | solution.py:189
  323.2 45.5 %reduce-scatter.11.cloned.1.call-done = bf16[1,256,1152]{2,1,0:T(8,128)(2,1)} async-done(((bf16[4,256,1152]{2,1,0:T(8,128)(2,1)}), bf16[1,256,1152]{2,1,0:T(8,128)(2,1)}) %reduce-scatter.11.cloned.1.call-update) | async-done | bytes 589840 | tf_op jit(solution)/shard_map/reduce_scatter | solution.py:165
  368.7 4.1 multiply_reduce_fusion.5
  375.4 11.2 %reduce-scatter.23.cloned.1.call-start = ((), (), s32[]{:S(2)}) async-start(), calls=%async_computation.21 | async-start | bytes 1990656 | tf_op jit(solution)/shard_map/reduce_scatter | solution.py:317
  386.6 5.4 fusion.4
  392.1 8.2 %bitcast_convert_fusion = bf16[1152,2,768]{2,0,1:T(8,128)(2,1)} fusion(bf16[4,256,1152]{2,1,0:T(8,128)(2,1)} %all-gather.9.cloned.1.call-done, bf16[4,256,1,768]{3,1,0,2:T(8,128)(2,1)} %copy-done.82, bf16[4,256,1,768]{3,1,0,2:T(8,128)(2,1)} %copy-done.81), kind=kOutput, calls=%fused_computation.1 | convolution fusion | flops 3631939584 | bytes 9043968 | tf_op jit(solution)/shard_map/bld,blkf->dkf/dot_general | solution.py:185
  400.4 24.6 %all-gather.13.cloned.1.call-done = bf16[4,256,1152]{2,1,0:T(8,128)(2,1)} async-done(((bf16[1,256,1152]{2,1,0:T(8,128)(2,1)}), bf16[4,256,1152]{2,1,0:T(8,128)(2,1)}) %all-gather.13.cloned.1.call-update) | async-done | bytes 2359312 | tf_op jit(solution)/shard_map/all_gather | solution.py:202
  445.4 3.5 convolution_convert_fusion.2
  449.8 5.3 bitcast_convert_fusion.1
  455.4 6.5 bitcast_convert_fusion.2
  461.9 4.4 reduce-scatter.23.cloned.1.call-done
  468.1 49.6 %reduce-scatter.21.cloned.1.call-done = bf16[144,2,768]{2,0,1:T(8,128)(2,1)} async-done(((bf16[1152,2,768]{2,0,1:T(8,128)(2,1)}), bf16[144,2,768]{2,0,1:T(8,128)(2,1)}) %reduce-scatter.21.cloned.1.call-update) | async-done | bytes 442384 | tf_op jit(solution)/shard_map/reduce_scatter | solution.py:317
  520.0 35.5 %reduce-scatter.19.cloned.1.call-done = bf16[288,144]{0,1:T(8,128)(2,1)} async-done(((bf16[288,1152]{0,1:T(8,128)(2,1)}), bf16[288,144]{0,1:T(8,128)(2,1)}) %reduce-scatter.19.cloned.1.call-update) | async-done | bytes 82960 | tf_op jit(solution)/shard_map/reduce_scatter | solution.py:317
  557.0 44.9 %reduce-scatter.17.cloned.1.call-done = bf16[144,3,288]{2,0,1:T(8,128)(2,1)} async-done(((bf16[1152,3,288]{2,0,1:T(8,128)(2,1)}), bf16[144,3,288]{2,0,1:T(8,128)(2,1)}) %reduce-scatter.17.cloned.1.call-update) | async-done | bytes 248848 | tf_op jit(solution)/shard_map/reduce_scatter | solution.py:317
  603.8 48.0 %reduce-scatter.15.cloned.1.call-done = bf16[1,256,1152]{2,1,0:T(8,128)(2,1)} async-done(((bf16[4,256,1152]{2,1,0:T(8,128)(2,1)}), bf16[1,256,1152]{2,1,0:T(8,128)(2,1)}) %reduce-scatter.15.cloned.1.call-update) | async-done | bytes 589840 | tf_op jit(solution)/shard_map/reduce_scatter | solution.py:241
  656.5 7.7 %reduce.26 = bf16[1152,6]{1,0:T(8,128)(2,1)S(1)} reduce(bf16[1152,1,6]{2,1,0:T(2,128)(2,1)} %bitcast.210, bf16[]{:T(256)} %broadcast.432), dimensions={1}, to_apply=%bitcast.178.reduce_sub_computation | reduce | bytes 27650
  665.2 3.3 all-to-all-start.1
  675.8 39.6 %psum.14 = f32[9360]{0:T(1024)S(1)} all-reduce(f32[9360]{0:T(1024)S(1)} %concatenate.23), channel_id=1, replica_groups=mesh['dp'=8,'tensor'=4] {'dp','tensor'}, use_global_device_ids=true, to_apply=%region_31.32 | all-reduce | flops 9360 | bytes 74880 | tf_op jit(solution)/shard_map/psum | solution.py:308
  719.4 17.1 %psum.15 = f32[4,1152]{1,0:T(4,128)S(1)} all-reduce(f32[4,1152]{1,0:T(4,128)S(1)} %convolution_bitcast_fusion.2), channel_id=1, replica_groups=mesh['dp'=8,'tensor'=4] {'tensor'}, use_global_device_ids=true, to_apply=%region_35.36 | all-reduce | flops 4608 | bytes 36864 | tf_op jit(solution)/shard_map/psum | solution.py:271
  737.5 10.0 %all-gather.1 = bf16[8,4,2880]{2,1,0:T(4,128)(2,1)S(1)} all-gather(bf16[1,4,2880]{2,1,0:T(4,128)(2,1)S(1)} %maximum_bitcast_fusion), channel_id=1, replica_groups=mesh['dp'=8,'tensor'=4] {'dp'}, dimensions={0}, use_global_device_ids=true | all-gather | bytes 207360 | tf_op jit(solution)/shard_map/all_gather | solution.py:274
  (309 shorter events, 100.1 us)
Async XLA Ops:
  7.2 19.0 %copy-start = (bf16[1152,1152]{1,0:T(8,128)(2,1)S(1)}, bf16[1152,1152]{1,0:T(8,128)(2,1)}, u32[]{:S(2)}) copy-start(bf16[1152,1152]{1,0:T(8,128)(2,1)} %param.37) | copy-start | bytes 7962628
  21.4 6.0 copy-start.54
  21.4 6.0 copy-start.56
  27.4 6.9 copy-start.3
  29.4 10.5 %all-to-all-start = ((bf16[4,6,288]{2,1,0:T(8,128)(2,1)}), bf16[4,6,288]{2,1,0:T(8,128)(2,1)S(1)}, u32[]{:S(2)}, u32[]{:S(2)}) async-start(bf16[4,6,288]{2,1,0:T(8,128)(2,1)} %copy.133), calls=%async_computation | async-start | bytes 49152 | tf_op jit(solution)/shard_map/all_to_all | solution.py:114
  34.3 55.7 %all-gather.7.cloned.1.call-start = ((), (), s32[]{:S(2)}) async-start(), calls=%async_computation.10 | async-start | bytes 2949120 | tf_op jit(solution)/shard_map/all_gather | solution.py:122
  34.4 8.0 %copy-start.58 = (f32[256]{0:T(256)}, f32[256]{0:T(256)S(1)}, u32[]{:S(2)}) copy-start(f32[256]{0:T(256)S(1)} %broadcast_multiply_fusion.5) | copy-start | bytes 3076
  34.8 7.7 %copy-start.79 = (bf16[72]{0:T(256)(128)(2,1)S(1)}, bf16[72]{0:T(256)(128)(2,1)}, u32[]{:S(2)}) copy-start(bf16[72]{0:T(256)(128)(2,1)} %param.26) | copy-start | bytes 436
  34.8 7.7 %copy-start.80 = (bf16[72]{0:T(256)(128)(2,1)S(1)}, bf16[72]{0:T(256)(128)(2,1)}, u32[]{:S(2)}) copy-start(bf16[72]{0:T(256)(128)(2,1)} %param.27) | copy-start | bytes 436
  34.8 59.9 %copy-start.61 = (f32[256]{0:T(256)}, f32[256]{0:T(256)S(1)}, u32[]{:S(2)}) copy-start(f32[256]{0:T(256)S(1)} %add_rsqrt_fusion.1) | copy-start | bytes 3076
  42.4 110.7 %reduce-scatter.9.cloned.1.call-start = ((), (), s32[]{:S(2)}) async-start(), calls=%async_computation.11 | async-start | bytes 2949120 | tf_op jit(solution)/shard_map/reduce_scatter | solution.py:146
  42.5 52.8 %copy-start.68 = (f32[72]{0:T(128)}, f32[72]{0:T(128)S(1)}, u32[]{:S(2)}) copy-start(f32[72]{0:T(128)S(1)} %convert_element_type.306) | copy-start | bytes 868
  42.5 53.9 %copy-start.70 = (f32[72]{0:T(128)}, f32[72]{0:T(128)S(1)}, u32[]{:S(2)}) copy-start(f32[72]{0:T(128)S(1)} %convert_element_type.309) | copy-start | bytes 868
  106.5 99.9 %all-gather.9.cloned.1.call-start = ((), (), s32[]{:S(2)}) async-start(), calls=%async_computation.12 | async-start | bytes 2949120 | tf_op jit(solution)/shard_map/all_gather | solution.py:157
  156.9 100.3 %all-gather.11.cloned.1.call-start = ((), (), s32[]{:S(2)}) async-start(), calls=%async_computation.14 | async-start | bytes 2949120 | tf_op jit(solution)/shard_map/all_gather | solution.py:177
  160.3 159.2 %reduce-scatter.13.cloned.1.call-start = ((), (), s32[]{:S(2)}) async-start(), calls=%async_computation.15 | async-start | bytes 2949120 | tf_op jit(solution)/shard_map/reduce_scatter | solution.py:189
  257.2 10.0 %copy-start.75 = (bf16[1152,2,768]{2,1,0:T(2,128)(2,1)S(1)}, bf16[1152,2,768]{2,1,0:T(2,128)(2,1)}, u32[]{:S(2)}) copy-start(bf16[1152,2,768]{2,1,0:T(2,128)(2,1)} %param.30) | copy-start | bytes 10616836
  272.8 95.9 %reduce-scatter.11.cloned.1.call-start = ((), (), s32[]{:S(2)}) async-start(), calls=%async_computation.13 | async-start | bytes 2949120 | tf_op jit(solution)/shard_map/reduce_scatter | solution.py:165
  278.5 146.5 %all-gather.13.cloned.1.call-start = ((), (), s32[]{:S(2)}) async-start(), calls=%async_computation.16 | async-start | bytes 2949120 | tf_op jit(solution)/shard_map/all_gather | solution.py:202
  375.4 90.9 %reduce-scatter.23.cloned.1.call-start = ((), (), s32[]{:S(2)}) async-start(), calls=%async_computation.21 | async-start | bytes 1990656 | tf_op jit(solution)/shard_map/reduce_scatter | solution.py:317
  392.0 125.7 %reduce-scatter.21.cloned.1.call-start = ((), (), s32[]{:S(2)}) async-start(), calls=%async_computation.20 | async-start | bytes 3981312 | tf_op jit(solution)/shard_map/reduce_scatter | solution.py:317
  400.3 155.1 %reduce-scatter.19.cloned.1.call-start = ((), (), s32[]{:S(2)}) async-start(), calls=%async_computation.19 | async-start | bytes 995328 | tf_op jit(solution)/shard_map/reduce_scatter | solution.py:317
  443.3 158.7 %reduce-scatter.17.cloned.1.call-start = ((), (), s32[]{:S(2)}) async-start(), calls=%async_computation.18 | async-start | bytes 2985984 | tf_op jit(solution)/shard_map/reduce_scatter | solution.py:317
  455.1 196.7 %reduce-scatter.15.cloned.1.call-start = ((), (), s32[]{:S(2)}) async-start(), calls=%async_computation.17 | async-start | bytes 2949120 | tf_op jit(solution)/shard_map/reduce_scatter | solution.py:241
  461.9 6.2 copy-start.64
  461.9 6.2 copy-start.63
  461.9 6.2 copy-start.67
  461.9 6.2 copy-start.66
  468.1 183.7 %copy-start.48 = (f32[1152]{0:T(1024)S(1)}, f32[1152]{0:T(1024)}, u32[]{:S(2)}) copy-start(f32[1152]{0:T(1024)} %copy-done.47) | copy-start | bytes 13828
  468.1 183.7 %copy-start.59 = (f32[256]{0:T(256)S(1)}, f32[256]{0:T(256)}, u32[]{:S(2)}) copy-start(f32[256]{0:T(256)} %copy-done.58) | copy-start | bytes 3076
  468.1 183.7 %copy-start.62 = (f32[256]{0:T(256)S(1)}, f32[256]{0:T(256)}, u32[]{:S(2)}) copy-start(f32[256]{0:T(256)} %copy-done.61) | copy-start | bytes 3076
  665.2 8.8 %all-to-all-start.1 = ((bf16[4,2,864]{2,1,0:T(2,128)(2,1)}), bf16[4,2,864]{2,1,0:T(2,128)(2,1)S(1)}, u32[]{:S(2)}, u32[]{:S(2)}) async-start(bf16[4,2,864]{2,1,0:T(2,128)(2,1)} %reshape.475), calls=%async_computation.6 | async-start | bytes 28672 | tf_op jit(solution)/shard_map/all_to_all | solution.py:264
  (65 other events, 135.1 us)
Sparse Core Ops, SparseCore 0:
  42.5 47.3 all-gather.6
  106.6 46.4 reduce-scatter.8
  157.0 49.3 all-gather.8
  208.4 48.7 all-gather.10
  272.9 46.4 reduce-scatter.12
  321.6 47.0 reduce-scatter.10
  375.5 49.3 all-gather.12
  428.3 37.9 reduce-scatter.22
  469.8 47.8 reduce-scatter.20
  520.8 34.6 reduce-scatter.18
  558.9 42.9 reduce-scatter.16
  604.1 47.6 reduce-scatter.14
where the time goes:
time: 774 us; the launch traced here: 764 us
  waiting for transfers between devices  480 us (62%)
  matrix products  92 us (12%)
  blocking collectives  77.2 us (10%)
  other arithmetic  53.3 us (7%)
  local copies, waits for them, and re-layouts  25.5 us (3%)
  starting transfers between devices  20.2 us (3%)
  between operations  16.4 us (2%)
    reduce_scatter x4, waiting for transfers between devices, scatter(): lax.psum_scatter(value, 'dp', scatter_dimension=axis, tiled=True)  134 us
    reduce_scatter x1, waiting for transfers between devices, shards(): lax.psum_scatter(jnp.einsum('blke,dke->bld', piece, project_weight, prefe...  48 us
    all_gather x1, waiting for transfers between devices, shards(): lax.all_gather((normed_local * (1.0 + attend_scale) + attend_shift).astyp...  47.1 us
    all_gather x1, waiting for transfers between devices, shards(): mod_two_all = lax.all_gather(mod_two, 'tensor', axis=0, tiled=True)  45.8 us
    reduce_scatter x1, waiting for transfers between devices, shards(): lax.psum_scatter(jnp.einsum('blf,fd->bld', piece, down_weight, preferred_...  45.5 us
    reduce_scatter x1, waiting for transfers between devices, shards(): lax.psum_scatter(jnp.einsum('blh,hd->bld', piece, output_weight, preferre...  45.3 us
    all_gather x1, waiting for transfers between devices, shards(): piece = lax.all_gather(branch_grad, 'tensor', axis=0, tiled=True)  41.2 us
    psum x1, blocking collectives, shards(): small = lax.psum(small, ('dp', 'tensor'))  39.6 us
  transfers between devices with their start and end apart: 14, of which 14 were waited for; matrix products, arithmetic and copies ran while one was open for 11% of the time, Pallas kernels for 0%

commit v1 on v0

--- a/solution.py
+++ b/solution.py
@@ -119,11 +119,17 @@
     positions = jnp.arange(length)
     token_local = tokens.astype(jnp.float32)
     normed_local, inverse_local = layer_norm(token_local)
-    mod_in = lax.all_gather(
-        (normed_local * (1.0 + attend_scale) + attend_shift).astype(jnp.bfloat16),
-        "tensor",
+    mod_in = jnp.concatenate(
+        lax.all_to_all(
+            jnp.stack(
+                [(normed_local * (1.0 + attend_scale) + attend_shift).astype(jnp.bfloat16)]
+                * lax.axis_size("tensor")
+            ),
+            "tensor",
+            0,
+            0,
+        ),
         axis=0,
-        tiled=True,
     )
     projected = jnp.einsum(
         "bld,dke->blke", mod_in, project_weight, preferred_element_type=jnp.float32

time: 774 us -> 783 us (1.012)
    all_to_all x0 -> x1, waiting for transfers between devices: none -> 52.8 us  [shards(): lax.all_to_all(jnp.stack([(normed_local * (1.0 + attend_scale) + attend_s...]
    all_gather x1 -> x0, waiting for transfers between devices: 47.1 us -> none  [shards(): lax.all_gather((normed_local * (1.0 + attend_scale) + attend_shift).astyp...]
    unnamed x172 -> x170, local copies, waits for them, and re-layouts: 17.4 us -> 17 us
  transfers between devices with their start and end apart: 14 -> 14, of which waited for: 14 -> 14; matrix products, arithmetic and copies ran while one was open for 11% -> 10% of each run, Pallas kernels for 0% -> 0%
where the time goes in v1:
time: 783 us; the launch traced here: 773 us
  waiting for transfers between devices  486 us (62%)
  matrix products  91.1 us (12%)
  blocking collectives  77.2 us (10%)
  other arithmetic  52 us (7%)
  local copies, waits for them, and re-layouts  26.5 us (3%)
  starting transfers between devices  24.9 us (3%)
  between operations  16 us (2%)
    reduce_scatter x4, waiting for transfers between devices, scatter(): lax.psum_scatter(value, 'dp', scatter_dimension=axis, tiled=True)  135 us
    all_to_all x1, waiting for transfers between devices, shards(): lax.all_to_all(jnp.stack([(normed_local * (1.0 + attend_scale) + attend_s...  52.8 us
    reduce_scatter x1, waiting for transfers between devices, shards(): lax.psum_scatter(jnp.einsum('blke,dke->bld', piece, project_weight, prefe...  48.2 us
    all_gather x1, waiting for transfers between devices, shards(): mod_two_all = lax.all_gather(mod_two, 'tensor', axis=0, tiled=True)  45.8 us
    reduce_scatter x1, waiting for transfers between devices, shards(): lax.psum_scatter(jnp.einsum('blf,fd->bld', piece, down_weight, preferred_...  45.5 us
    reduce_scatter x1, waiting for transfers between devices, shards(): lax.psum_scatter(jnp.einsum('blh,hd->bld', piece, output_weight, preferre...  44.7 us
    all_gather x1, waiting for transfers between devices, shards(): piece = lax.all_gather(branch_grad, 'tensor', axis=0, tiled=True)  41.3 us
    reduce_scatter x1, waiting for transfers between devices, shards(): lax.psum_scatter(jnp.einsum('blkf,dkf->bld', piece, expand_weight, prefer...  39.6 us
  transfers between devices with their start and end apart: 14, of which 14 were waited for; matrix products, arithmetic and copies ran while one was open for 10% of the time, Pallas kernels for 0%

profile of v1, /device:TPU:0, one launch (start us, length us, event | category | flops | bytes accessed | tf_op | source)
XLA Modules:
  0.0 773.2 jit_solution(13817582369526632306)
XLA Ops:
  8.1 10.4 %all-gather = s32[8,4,2]{1,2,0:T(2,128)S(1)} all-gather(s32[1,4,2]{1,2,0:T(2,128)S(1)} %add_bitcast_fusion), channel_id=1, replica_groups=mesh['dp'=8,'tensor'=4] {'dp'}, dimensions={0}, use_global_device_ids=true | all-gather | bytes 288 | tf_op jit(solution)/shard_map/all_gather | solution.py:94
  29.4 4.9 all-to-all-start
  34.8 5.1 all-to-all-done
  43.2 4.6 all-to-all-start.1
  48.2 52.8 %all-to-all-done.1 = bf16[4,1,256,1152]{3,2,1,0:T(8,128)(2,1)} async-done(((bf16[4,1,256,1152]{3,2,1,0:T(8,128)(2,1)}), bf16[4,1,256,1152]{3,2,1,0:T(8,128)(2,1)}, u32[]{:S(2)}, u32[]{:S(2)}) %all-to-all-start.1) | async-done | bytes 2359328 | tf_op jit(solution)/shard_map/all_to_all | solution.py:123
  101.1 4.8 fusion.10
  117.4 44.7 %reduce-scatter.9.cloned.1.call-done = bf16[1,256,1152]{2,1,0:T(8,128)(2,1)} async-done(((bf16[4,256,1152]{2,1,0:T(8,128)(2,1)}), bf16[1,256,1152]{2,1,0:T(8,128)(2,1)}) %reduce-scatter.9.cloned.1.call-update) | async-done | bytes 589840 | tf_op jit(solution)/shard_map/reduce_scatter | solution.py:152
  169.5 45.8 %all-gather.6.cloned.1.call-done = bf16[4,256,1152]{2,1,0:T(8,128)(2,1)} async-done(((bf16[1,256,1152]{2,1,0:T(8,128)(2,1)}), bf16[4,256,1152]{2,1,0:T(8,128)(2,1)}) %all-gather.6.cloned.1.call-update) | async-done | bytes 2359312 | tf_op jit(solution)/shard_map/all_gather | solution.py:163
  215.4 9.6 %fusion.1 = f32[4,256,2,768]{3,1,2,0:T(8,128)} fusion(bf16[1152,2,768]{2,1,0:T(2,128)(2,1)} %param.30, bf16[4,256,1152]{2,1,0:T(8,128)(2,1)} %all-gather.6.cloned.1.call-done), kind=kOutput, calls=%fused_computation.14 | convolution fusion | flops 3623878656 | bytes 12189696 | tf_op jit(solution)/shard_map/bld,dkf->blkf/dot_general | solution.py:164
  224.9 41.3 %all-gather.8.cloned.1.call-done = bf16[4,256,1152]{2,1,0:T(8,128)(2,1)} async-done(((bf16[1,256,1152]{2,1,0:T(8,128)(2,1)}), bf16[4,256,1152]{2,1,0:T(8,128)(2,1)}) %all-gather.8.cloned.1.call-update) | async-done | bytes 2359312 | tf_op jit(solution)/shard_map/all_gather | solution.py:183
  266.3 8.4 %fusion.25 = (bf16[4,256,1,768]{3,1,0,2:T(8,128)(2,1)S(1)}, bf16[4,256,1,768]{3,1,0,2:T(8,128)(2,1)S(1)}, bf16[4,256,768]{2,1,0:T(8,128)(2,1)}) fusion(f32[4,256,2,768]{3,1,2,0:T(8,128)} %fusion.1, bf16[4,256,1152]{2,1,0:T(8,128)(2,1)} %all-gather.8.cloned.1.call-done, bf16[768,1152]{1,0:T(8,128)(2,1)} %param.31), kind=kOutput, calls=%fused_computation.61 | convolution fusion | flops 1823735808 | bytes 15138816 | tf_op jit(solution)/shard_map/bld,fd->blf/dot_general | solution.py:185
  276.3 5.6 bitcast_convert_fusion.3
  282.0 5.6 convolution_convert_fusion
  288.9 39.6 %reduce-scatter.13.cloned.1.call-done = bf16[1,256,1152]{2,1,0:T(8,128)(2,1)} async-done(((bf16[4,256,1152]{2,1,0:T(8,128)(2,1)}), bf16[1,256,1152]{2,1,0:T(8,128)(2,1)}) %reduce-scatter.13.cloned.1.call-update) | async-done | bytes 589840 | tf_op jit(solution)/shard_map/reduce_scatter | solution.py:195
  332.3 45.5 %reduce-scatter.11.cloned.1.call-done = bf16[1,256,1152]{2,1,0:T(8,128)(2,1)} async-done(((bf16[4,256,1152]{2,1,0:T(8,128)(2,1)}), bf16[1,256,1152]{2,1,0:T(8,128)(2,1)}) %reduce-scatter.11.cloned.1.call-update) | async-done | bytes 589840 | tf_op jit(solution)/shard_map/reduce_scatter | solution.py:171
  377.8 4.1 multiply_reduce_fusion.5
  384.5 11.3 %reduce-scatter.23.cloned.1.call-start = ((), (), s32[]{:S(2)}) async-start(), calls=%async_computation.21 | async-start | bytes 1990656 | tf_op jit(solution)/shard_map/reduce_scatter | solution.py:323
  395.8 5.4 fusion.4
  401.3 8.2 %bitcast_convert_fusion = bf16[1152,2,768]{2,0,1:T(8,128)(2,1)} fusion(bf16[4,256,1152]{2,1,0:T(8,128)(2,1)} %all-gather.6.cloned.1.call-done, bf16[4,256,1,768]{3,1,0,2:T(8,128)(2,1)} %copy-done.81, bf16[4,256,1,768]{3,1,0,2:T(8,128)(2,1)} %copy-done.80), kind=kOutput, calls=%fused_computation.1 | convolution fusion | flops 3631939584 | bytes 9043968 | tf_op jit(solution)/shard_map/bld,blkf->dkf/dot_general | solution.py:191
  409.6 24.4 %all-gather.10.cloned.1.call-done = bf16[4,256,1152]{2,1,0:T(8,128)(2,1)} async-done(((bf16[1,256,1152]{2,1,0:T(8,128)(2,1)}), bf16[4,256,1152]{2,1,0:T(8,128)(2,1)}) %all-gather.10.cloned.1.call-update) | async-done | bytes 2359312 | tf_op jit(solution)/shard_map/all_gather | solution.py:208
  456.6 7.0 bitcast_convert_fusion.1
  463.9 6.5 bitcast_convert_fusion.2
  470.5 5.0 reduce-scatter.23.cloned.1.call-done
  477.3 49.5 %reduce-scatter.21.cloned.1.call-done = bf16[144,2,768]{2,0,1:T(8,128)(2,1)} async-done(((bf16[1152,2,768]{2,0,1:T(8,128)(2,1)}), bf16[144,2,768]{2,0,1:T(8,128)(2,1)}) %reduce-scatter.21.cloned.1.call-update) | async-done | bytes 442384 | tf_op jit(solution)/shard_map/reduce_scatter | solution.py:323
  529.1 35.7 %reduce-scatter.19.cloned.1.call-done = bf16[288,144]{0,1:T(8,128)(2,1)} async-done(((bf16[288,1152]{0,1:T(8,128)(2,1)}), bf16[288,144]{0,1:T(8,128)(2,1)}) %reduce-scatter.19.cloned.1.call-update) | async-done | bytes 82960 | tf_op jit(solution)/shard_map/reduce_scatter | solution.py:323
  566.3 44.7 %reduce-scatter.17.cloned.1.call-done = bf16[144,3,288]{2,0,1:T(8,128)(2,1)} async-done(((bf16[1152,3,288]{2,0,1:T(8,128)(2,1)}), bf16[144,3,288]{2,0,1:T(8,128)(2,1)}) %reduce-scatter.17.cloned.1.call-update) | async-done | bytes 248848 | tf_op jit(solution)/shard_map/reduce_scatter | solution.py:323
  612.9 48.2 %reduce-scatter.15.cloned.1.call-done = bf16[1,256,1152]{2,1,0:T(8,128)(2,1)} async-done(((bf16[4,256,1152]{2,1,0:T(8,128)(2,1)}), bf16[1,256,1152]{2,1,0:T(8,128)(2,1)}) %reduce-scatter.15.cloned.1.call-update) | async-done | bytes 589840 | tf_op jit(solution)/shard_map/reduce_scatter | solution.py:247
  665.8 7.7 reduce.26
  674.5 3.3 all-to-all-start.2
  685.1 39.6 %psum.14 = f32[9360]{0:T(1024)S(1)} all-reduce(f32[9360]{0:T(1024)S(1)} %concatenate.23), channel_id=1, replica_groups=mesh['dp'=8,'tensor'=4] {'dp','tensor'}, use_global_device_ids=true, to_apply=%region_31.32 | all-reduce | flops 9360 | bytes 74880 | tf_op jit(solution)/shard_map/psum | solution.py:314
  728.7 17.1 %psum.15 = f32[4,1152]{1,0:T(4,128)S(1)} all-reduce(f32[4,1152]{1,0:T(4,128)S(1)} %convolution_bitcast_fusion.2), channel_id=1, replica_groups=mesh['dp'=8,'tensor'=4] {'tensor'}, use_global_device_ids=true, to_apply=%region_35.36 | all-reduce | flops 4608 | bytes 36864 | tf_op jit(solution)/shard_map/psum | solution.py:277
  746.8 10.0 %all-gather.1 = bf16[8,4,2880]{2,1,0:T(4,128)(2,1)S(1)} all-gather(bf16[1,4,2880]{2,1,0:T(4,128)(2,1)S(1)} %maximum_bitcast_fusion), channel_id=1, replica_groups=mesh['dp'=8,'tensor'=4] {'dp'}, dimensions={0}, use_global_device_ids=true | all-gather | bytes 207360 | tf_op jit(solution)/shard_map/all_gather | solution.py:280
  (302 shorter events, 100.5 us)
Async XLA Ops:
  7.2 19.0 %copy-start = (bf16[1152,1152]{1,0:T(8,128)(2,1)S(1)}, bf16[1152,1152]{1,0:T(8,128)(2,1)}, u32[]{:S(2)}) copy-start(bf16[1152,1152]{1,0:T(8,128)(2,1)} %param.37) | copy-start | bytes 7962628
  21.4 6.0 copy-start.54
  21.4 6.0 copy-start.56
  27.4 6.9 copy-start.4
  29.4 10.5 %all-to-all-start = ((bf16[4,6,288]{2,1,0:T(8,128)(2,1)}), bf16[4,6,288]{2,1,0:T(8,128)(2,1)S(1)}, u32[]{:S(2)}, u32[]{:S(2)}) async-start(bf16[4,6,288]{2,1,0:T(8,128)(2,1)} %copy.125), calls=%async_computation | async-start | bytes 49152 | tf_op jit(solution)/shard_map/all_to_all | solution.py:114
  34.4 8.8 %copy-start.58 = (f32[256]{0:T(256)}, f32[256]{0:T(256)S(1)}, u32[]{:S(2)}) copy-start(f32[256]{0:T(256)S(1)} %broadcast_multiply_fusion.5) | copy-start | bytes 3076
  34.8 8.4 %copy-start.61 = (f32[256]{0:T(256)}, f32[256]{0:T(256)S(1)}, u32[]{:S(2)}) copy-start(f32[256]{0:T(256)S(1)} %add_rsqrt_fusion.1) | copy-start | bytes 3076
  43.2 57.9 %all-to-all-start.1 = ((bf16[4,1,256,1152]{3,2,1,0:T(8,128)(2,1)}), bf16[4,1,256,1152]{3,2,1,0:T(8,128)(2,1)}, u32[]{:S(2)}, u32[]{:S(2)}) async-start(bf16[4,1,256,1152]{3,2,1,0:T(8,128)(2,1)} %stack.64), calls=%async_computation.1 | async-start | bytes 4718592 | tf_op jit(solution)/shard_map/all_to_all | solution.py:123
  47.8 114.2 %reduce-scatter.9.cloned.1.call-start = ((), (), s32[]{:S(2)}) async-start(), calls=%async_computation.11 | async-start | bytes 2949120 | tf_op jit(solution)/shard_map/reduce_scatter | solution.py:152
  47.9 58.2 %copy-start.68 = (f32[72]{0:T(128)}, f32[72]{0:T(128)S(1)}, u32[]{:S(2)}) copy-start(f32[72]{0:T(128)S(1)} %convert_element_type.309) | copy-start | bytes 868
  48.0 58.2 %copy-start.70 = (f32[72]{0:T(128)}, f32[72]{0:T(128)S(1)}, u32[]{:S(2)}) copy-start(f32[72]{0:T(128)S(1)} %convert_element_type.312) | copy-start | bytes 868
  116.1 99.3 %all-gather.6.cloned.1.call-start = ((), (), s32[]{:S(2)}) async-start(), calls=%async_computation.12 | async-start | bytes 2949120 | tf_op jit(solution)/shard_map/all_gather | solution.py:163
  165.8 100.4 %all-gather.8.cloned.1.call-start = ((), (), s32[]{:S(2)}) async-start(), calls=%async_computation.14 | async-start | bytes 2949120 | tf_op jit(solution)/shard_map/all_gather | solution.py:183
  169.2 159.3 %reduce-scatter.13.cloned.1.call-start = ((), (), s32[]{:S(2)}) async-start(), calls=%async_computation.15 | async-start | bytes 2949120 | tf_op jit(solution)/shard_map/reduce_scatter | solution.py:195
  266.3 10.0 %copy-start.75 = (bf16[1152,2,768]{2,1,0:T(2,128)(2,1)S(1)}, bf16[1152,2,768]{2,1,0:T(2,128)(2,1)}, u32[]{:S(2)}) copy-start(bf16[1152,2,768]{2,1,0:T(2,128)(2,1)} %param.30) | copy-start | bytes 10616836
  281.9 95.9 %reduce-scatter.11.cloned.1.call-start = ((), (), s32[]{:S(2)}) async-start(), calls=%async_computation.13 | async-start | bytes 2949120 | tf_op jit(solution)/shard_map/reduce_scatter | solution.py:171
  287.6 146.5 %all-gather.10.cloned.1.call-start = ((), (), s32[]{:S(2)}) async-start(), calls=%async_computation.16 | async-start | bytes 2949120 | tf_op jit(solution)/shard_map/all_gather | solution.py:208
  384.5 90.9 %reduce-scatter.23.cloned.1.call-start = ((), (), s32[]{:S(2)}) async-start(), calls=%async_computation.21 | async-start | bytes 1990656 | tf_op jit(solution)/shard_map/reduce_scatter | solution.py:323
  401.2 125.6 %reduce-scatter.21.cloned.1.call-start = ((), (), s32[]{:S(2)}) async-start(), calls=%async_computation.20 | async-start | bytes 3981312 | tf_op jit(solution)/shard_map/reduce_scatter | solution.py:323
  409.5 155.2 %reduce-scatter.19.cloned.1.call-start = ((), (), s32[]{:S(2)}) async-start(), calls=%async_computation.19 | async-start | bytes 995328 | tf_op jit(solution)/shard_map/reduce_scatter | solution.py:323
  451.1 160.0 %reduce-scatter.17.cloned.1.call-start = ((), (), s32[]{:S(2)}) async-start(), calls=%async_computation.18 | async-start | bytes 2985984 | tf_op jit(solution)/shard_map/reduce_scatter | solution.py:323
  463.7 197.5 %reduce-scatter.15.cloned.1.call-start = ((), (), s32[]{:S(2)}) async-start(), calls=%async_computation.17 | async-start | bytes 2949120 | tf_op jit(solution)/shard_map/reduce_scatter | solution.py:247
  470.4 6.7 copy-start.64
  470.4 6.7 copy-start.63
  470.4 6.8 copy-start.67
  470.4 6.8 copy-start.66
  477.2 183.9 %copy-start.48 = (f32[1152]{0:T(1024)S(1)}, f32[1152]{0:T(1024)}, u32[]{:S(2)}) copy-start(f32[1152]{0:T(1024)} %copy-done.47) | copy-start | bytes 13828
  477.2 183.9 %copy-start.59 = (f32[256]{0:T(256)S(1)}, f32[256]{0:T(256)}, u32[]{:S(2)}) copy-start(f32[256]{0:T(256)} %copy-done.58) | copy-start | bytes 3076
  477.2 183.9 %copy-start.62 = (f32[256]{0:T(256)S(1)}, f32[256]{0:T(256)}, u32[]{:S(2)}) copy-start(f32[256]{0:T(256)} %copy-done.61) | copy-start | bytes 3076
  674.5 8.8 %all-to-all-start.2 = ((bf16[4,2,864]{2,1,0:T(2,128)(2,1)}), bf16[4,2,864]{2,1,0:T(2,128)(2,1)S(1)}, u32[]{:S(2)}, u32[]{:S(2)}) async-start(bf16[4,2,864]{2,1,0:T(2,128)(2,1)} %reshape.481), calls=%async_computation.7 | async-start | bytes 28672 | tf_op jit(solution)/shard_map/all_to_all | solution.py:270
  756.8 5.2 copy-start.57
  756.9 6.0 copy-start.74
  (64 other events, 131.7 us)
Sparse Core Ops, SparseCore 0:
  116.2 45.8 reduce-scatter.8
  166.0 49.3 all-gather.5
  217.5 48.7 all-gather.7
  282.0 46.4 reduce-scatter.12
  330.7 47.0 reduce-scatter.10
  384.6 49.3 all-gather.9
  437.4 37.9 reduce-scatter.22
  478.9 47.8 reduce-scatter.20
  530.0 34.6 reduce-scatter.18
  568.1 42.9 reduce-scatter.16
  613.4 47.7 reduce-scatter.14
